TPU v7x, 16 devices: a whole 2x2x2 slice. The times are simulated.
16 devices in a mesh: rep: 1, r: 4 (over y, z), s: 4 (over x, core).
Axes of the slice: x: 2, y: 2, z: 2, core: 2. Of those that a mesh axis runs over, the one named last changes fastest.
Arguments:
- x: bfloat16 [16, 4096, 640], P(('rep', 'r', 's'))
- dy: bfloat16 [16, 4096, 640], P(('rep', 'r', 's'))
- w_gate: bfloat16 [2, 640, 3200], P(None, 's')
- w_up: bfloat16 [2, 640, 3200], P(None, 's')
- w_down: bfloat16 [2, 3200, 640], P(None, 's')
- m_w_gate: float32 [2, 640, 3200], P(None, 's')
- m_w_up: float32 [2, 640, 3200], P(None, 's')
- m_w_down: float32 [2, 3200, 640], P(None, 's')
- v_w_gate: float32 [2, 640, 3200], P(None, 's')
- v_w_up: float32 [2, 640, 3200], P(None, 's')
- v_w_down: float32 [2, 3200, 640], P(None, 's')
Outputs:
- output 1: bfloat16 [2, 640, 3200], P('rep', 's')
- output 2: bfloat16 [2, 640, 3200], P('rep', 's')
- output 3: bfloat16 [2, 3200, 640], P('rep', 's')
- output 4: float32 [2, 640, 3200], P('rep', 's')
- output 5: float32 [2, 640, 3200], P('rep', 's')
- output 6: float32 [2, 3200, 640], P('rep', 's')
- output 7: float32 [2, 640, 3200], P('rep', 's')
- output 8: float32 [2, 640, 3200], P('rep', 's')
- output 9: float32 [2, 3200, 640], P('rep', 's')
All inputs are finite; a program needn't handle non-finite values.
Results may differ from a plain program's by a relative error of at most 0.0223.
Values are sent between devices in bfloat16 or wider.
A program may use at most 2 GiB of HBM per device.

v0:
```python
import jax
import jax.numpy as jnp
from jax import lax
from jax.sharding import PartitionSpec as P

NAMES = ("w_gate", "w_up", "w_down")


def matmul(a, w):
    return jnp.dot(a, w, preferred_element_type=jnp.float32).astype(jnp.bfloat16)


def normed(h):
    wide = h.astype(jnp.float32)
    scale = lax.rsqrt(jnp.mean(wide**2, -1, keepdims=True) + 1e-6)
    return (wide * scale).astype(jnp.bfloat16)


def layer(h, w):
    a = normed(h)
    gate = jnp.dot(a, w["w_gate"], preferred_element_type=jnp.float32)
    up = jnp.dot(a, w["w_up"], preferred_element_type=jnp.float32)
    return h + matmul((jax.nn.silu(gate) * up).astype(jnp.bfloat16), w["w_down"])


def adamw(w, m, v, g):
    m = 0.9 * m + 0.1 * g
    v = 0.95 * v + 0.05 * g * g
    step = m * lax.rsqrt(v + 1e-8) + 0.1 * w
    return (w - 0.02 * step).astype(jnp.bfloat16), m, v


def solution(mesh):
    def fetched(weights, number):
        return {name: lax.all_gather(w[number], "s", axis=0, tiled=True) for name, w in zip(NAMES, weights, strict=True)}

    def summed(term):
        return lax.psum(lax.psum_scatter(term, "s", scatter_dimension=0, tiled=True), "r")

    def step(x, dy, *arrays):
        weights, m, v = (arrays[i : i + 3] for i in (0, 3, 6))
        layers = weights[0].shape[0]
        h, kept = x[0], []
        for number in range(layers):
            kept.append(h)
            h = layer(h, fetched(weights, number))
        by_h, mine = dy[0], [None] * layers
        for number in reversed(range(layers)):
            _, back = jax.vjp(lambda w, h: layer(h, w), fetched(weights, number), kept[number])
            by_w, by_h = back(by_h)
            mine[number] = [summed(by_w[name]) for name in NAMES]
        gradients = [jnp.stack([mine[number][i] for number in range(layers)]).astype(jnp.float32) for i in range(3)]
        new = [adamw(w.astype(jnp.float32), m, v, g) for w, m, v, g in zip(weights, m, v, gradients, strict=True)]
        return tuple(one[which] for which in range(3) for one in new)

    states, cut = P(("rep", "r", "s"), None, None), P(None, "s", None)
    return jax.shard_map(
        step,
        mesh=mesh,
        in_specs=(states, states) + (cut,) * 9,
        out_specs=(P("rep", "s", None),) * 9,
        check_vma=False,
    )
```

profile of v0, /device:TPU:0, one launch (start us, length us, event | category | flops | bytes accessed | tf_op | source)
XLA Modules:
  0.0 815.2 jit_solution(16222614881369836591)
XLA Ops:
  7.2 0.0 all-gather.13.cloned.1.call-start
  7.2 3.1 fusion.85
  10.4 0.0 all-gather.15.cloned.1.call-start
  10.4 3.0 fusion.84
  13.4 0.0 all-gather.17.cloned.1.call-start
  13.5 1.5 fusion.83
  15.0 0.0 all-gather.21.cloned.1.call-start
  15.0 0.5 all-gather.21.cloned.1.call-update
  15.5 0.0 all-gather.23.cloned.1.call-start
  15.6 0.5 all-gather.23.cloned.1.call-update
  16.2 0.5 all-gather.19.cloned.1.call-update
  16.7 0.0 reduce-scatter.15.cloned.1.call-start
  16.7 8.0 copy.20
  24.8 3.6 fusion.15
  28.4 7.9 copy.21
  36.4 8.8 %all-gather.13.cloned.1.call-done = bf16[1,640,3200]{2,1,0:T(8,128)(2,1)} async-done(((bf16[1,160,3200]{2,1,0:T(8,128)(2,1)}), bf16[1,640,3200]{2,1,0:T(8,128)(2,1)}) %all-gather.13.cloned.1.call-update) | async-done | bytes 4096016 | tf_op jit(solution)/shard_map/all_gather | solution.py:35
  45.2 29.3 %fusion.61 = f32[4096,3200]{1,0:T(8,128)} fusion(bf16[1,640,3200]{2,1,0:T(8,128)(2,1)} %all-gather.13.cloned.1.call-done, bf16[1,4096,640]{1,2,0:T(8,128)(2,1)} %copy.20, f32[4096]{0:T(1024)S(1)} %add_rsqrt_fusion), kind=kOutput, calls=%fused_computation.92 | convolution fusion | flops 16785080320 | bytes 61784064 | tf_op jit(solution)/shard_map/dot_general | solution.py:21
  74.5 4.7 all-gather.15.cloned.1.call-done
  79.2 50.9 %multiply_convert_fusion.1 = (bf16[4096,3200]{1,0:T(8,128)(2,1)}, f32[4096,3200]{1,0:T(8,128)}) fusion(f32[4096,3200]{1,0:T(8,128)} %fusion.61, bf16[1,640,3200]{2,1,0:T(8,128)(2,1)} %all-gather.15.cloned.1.call-done, bf16[1,4096,640]{1,2,0:T(8,128)(2,1)} %copy.20, f32[4096]{0:T(1024)S(1)} %add_rsqrt_fusion), kind=kOutput, calls=%fused_computation.17 | convolution fusion | flops 16863723520 | bytes 140427264 | tf_op jit(solution)/shard_map/dot_general | solution.py:22
  130.1 24.8 %fusion.19 = (f32[4096]{0:T(1024)S(1)}, bf16[4096,640]{0,1:T(8,128)(2,1)}) fusion(bf16[4096,3200]{1,0:T(8,128)(2,1)} %get-tuple-element.30, bf16[1,3200,640]{2,1,0:T(8,128)(2,1)} %all-gather.17.cloned.1.call-done, bf16[1,4096,640]{1,2,0:T(8,128)(2,1)} %copy.20), kind=kOutput, calls=%fused_computation.37 | convolution fusion | flops 16790319104 | bytes 40812544 | tf_op jit(solution)/shard_map/dot_general | solution.py:10
  154.9 0.6 copy-done.11
  155.5 28.1 %convolution_convert_fusion.1 = bf16[4096,3200]{1,0:T(8,128)(2,1)} fusion(bf16[1,4096,640]{2,1,0:T(8,128)(2,1)} %param.12, bf16[1,3200,640]{2,1,0:T(8,128)(2,1)} %all-gather.21.cloned.1.call-done), kind=kOutput, calls=%fused_computation.23 | convolution fusion | flops 16790323200 | bytes 35553280 | tf_op jit(solution)/shard_map/transpose(jvp())/dot_general | solution.py:10
  183.6 29.4 %fusion.50 = f32[4096,3200]{1,0:T(8,128)} fusion(bf16[1,640,3200]{2,1,0:T(8,128)(2,1)} %all-gather.23.cloned.1.call-done, bf16[4096,640]{0,1:T(8,128)(2,1)} %get-tuple-element.33, f32[4096]{0:T(1024)S(1)} %fusion.71), kind=kOutput, calls=%fused_computation.81 | convolution fusion | flops 16785080320 | bytes 61784064 | tf_op jit(solution)/shard_map/jvp()/dot_general | solution.py:22
  213.0 1.7 all-gather.19.cloned.1.call-done
  214.7 67.7 %fusion.2 = (bf16[4096,3200]{1,0:T(8,128)(2,1)}, f32[4096,3200]{1,0:T(8,128)}) fusion(f32[4096,3200]{1,0:T(8,128)} %fusion.50, bf16[4096,3200]{1,0:T(8,128)(2,1)} %convolution_convert_fusion.1, bf16[1,640,3200]{2,1,0:T(8,128)(2,1)} %all-gather.19.cloned.1.call-done, bf16[4096,640]{0,1:T(8,128)(2,1)} %get-tuple-element.33, f32[4096]{0:T(1024)S(1)} %fusion.71), kind=kOutput, calls=%fused_computation.8 | convolution fusion | flops 16942366720 | bytes 166641664 | tf_op jit(solution)/shard_map/jvp()/dot_general | solution.py:21
  282.4 22.8 %convolution_convert_fusion.4 = bf16[4096,640]{0,1:T(8,128)(2,1)} fusion(bf16[4096,3200]{1,0:T(8,128)(2,1)} %get-tuple-element.34, bf16[1,640,3200]{2,1,0:T(8,128)(2,1)S(1)} %copy-done.15), kind=kOutput, calls=%fused_computation.47 | convolution fusion | flops 16777216000 | bytes 35553280 | tf_op jit(solution)/shard_map/transpose(jvp())/dot_general | solution.py:21
  305.3 40.4 %fusion.21 = (f32[4096]{0:T(1024)S(1)}, bf16[4096,640]{0,1:T(8,128)(2,1)}) fusion(bf16[4096,640]{0,1:T(8,128)(2,1)} %get-tuple-element.33, bf16[4096,640]{0,1:T(8,128)(2,1)} %convolution_convert_fusion.4, bf16[1,640,3200]{2,1,0:T(8,128)(2,1)} %all-gather.23.cloned.1.call-done, bf16[4096,3200]{1,0:T(8,128)(2,1)} %convolution_convert_fusion.1, ...), kind=kOutput, calls=%fused_computation.39 | convolution fusion | flops 16871583744 | bytes 98484224 | tf_op jit(solution)/shard_map/transpose(jvp())/dot_general | solution.py:22
  345.7 11.9 %fusion.32 = bf16[4096,640]{0,1:T(8,128)(2,1)} fusion(bf16[4096,640]{0,1:T(8,128)(2,1)} %get-tuple-element.33, bf16[4096,640]{0,1:T(8,128)(2,1)} %get-tuple-element.37, bf16[1,4096,640]{1,2,0:T(8,128)(2,1)} %copy.21, f32[4096]{0:T(1024)S(1)} %multiply_multiply_fusion.3, f32[4096]{0:T(1024)S(1)} %fusion.71), kind=kLoop, calls=%fused_computation.54 | loop fusion | flops 18350080 | bytes 21004288 | tf_op jit(solution)/shard_map/transpose(jvp())/add_any | solution.py:14
  357.5 26.5 %convolution_convert_fusion.2 = bf16[3200,640]{1,0:T(8,128)(2,1)} fusion(bf16[4096,3200]{1,0:T(8,128)(2,1)} %get-tuple-element.30, bf16[4096,640]{0,1:T(8,128)(2,1)} %fusion.32), kind=kOutput, calls=%fused_computation.45 | convolution fusion | flops 16779264000 | bytes 35553280 | tf_op jit(solution)/shard_map/transpose(jvp())/dot_general | solution.py:10
  384.0 0.0 reduce-scatter.17.cloned.1.call-start
  384.1 39.4 %fusion.23 = bf16[3200,640]{1,0:T(8,128)(2,1)} fusion(f32[4096,3200]{1,0:T(8,128)} %fusion.50, bf16[1,4096,640]{2,1,0:T(8,128)(2,1)} %param.12, f32[4096,3200]{1,0:T(8,128)} %get-tuple-element.35), kind=kOutput, calls=%fused_computation.40 | convolution fusion | flops 16857907200 | bytes 114196480 | tf_op jit(solution)/shard_map/transpose(jvp())/dot_general | solution.py:10
  423.6 0.0 reduce-scatter.11.cloned.1.call-start
  423.6 27.4 %convolution_convert_fusion = bf16[4096,3200]{1,0:T(8,128)(2,1)} fusion(bf16[4096,640]{0,1:T(8,128)(2,1)} %fusion.32, bf16[1,3200,640]{2,1,0:T(8,128)(2,1)} %all-gather.17.cloned.1.call-done), kind=kOutput, calls=%fused_computation.22 | convolution fusion | flops 16790323200 | bytes 35553280 | tf_op jit(solution)/shard_map/transpose(jvp())/dot_general | solution.py:10
  451.0 34.6 %fusion.29 = bf16[640,3200]{1,0:T(8,128)(2,1)} fusion(bf16[4096,3200]{1,0:T(8,128)(2,1)} %convolution_convert_fusion, f32[4096,3200]{1,0:T(8,128)} %fusion.61, bf16[1,4096,640]{1,2,0:T(8,128)(2,1)} %copy.20, f32[4096]{0:T(1024)S(1)} %copy-done.14), kind=kOutput, calls=%fused_computation.44 | convolution fusion | flops 16865771520 | bytes 87998464 | tf_op jit(solution)/shard_map/transpose(jvp())/dot_general | solution.py:22
  485.7 0.0 reduce-scatter.13.cloned.1.call-start
  485.8 34.8 %fusion.25 = bf16[640,3200]{1,0:T(8,128)(2,1)} fusion(bf16[4096,3200]{1,0:T(8,128)(2,1)} %convolution_convert_fusion.1, bf16[4096,640]{0,1:T(8,128)(2,1)} %get-tuple-element.33, f32[4096]{0:T(1024)S(1)} %copy-done.9, f32[4096,3200]{1,0:T(8,128)} %get-tuple-element.35), kind=kOutput, calls=%fused_computation.42 | convolution fusion | flops 16865771520 | bytes 87998464 | tf_op jit(solution)/shard_map/transpose(jvp())/dot_general | solution.py:22
  520.6 0.0 reduce-scatter.7.cloned.1.call-start
  520.6 46.8 %fusion.26 = bf16[640,3200]{1,0:T(8,128)(2,1)} fusion(f32[4096,3200]{1,0:T(8,128)} %fusion.61, f32[4096,3200]{1,0:T(8,128)} %get-tuple-element.31, bf16[4096,3200]{1,0:T(8,128)(2,1)} %convolution_convert_fusion, bf16[1,4096,640]{1,2,0:T(8,128)(2,1)} %copy.20, f32[4096]{0:T(1024)S(1)} %copy-done.14), kind=kOutput, calls=%fused_computation.43 | convolution fusion | flops 16931307520 | bytes 140427264 | tf_op jit(solution)/shard_map/transpose(jvp())/dot_general | solution.py:21
  567.5 0.0 reduce-scatter.9.cloned.1.call-start
  567.6 26.2 %convolution_convert_fusion.3 = bf16[640,3200]{1,0:T(8,128)(2,1)} fusion(bf16[4096,3200]{1,0:T(8,128)(2,1)} %get-tuple-element.34, bf16[4096,640]{0,1:T(8,128)(2,1)} %get-tuple-element.33, f32[4096]{0:T(1024)S(1)} %copy-done.10), kind=kOutput, calls=%fused_computation.46 | convolution fusion | flops 16785080320 | bytes 35569664 | tf_op jit(solution)/shard_map/transpose(jvp())/dot_general | solution.py:21
  593.7 0.3 all-reduce.3.cloned.1.call-start
  594.2 16.3 %reduce-scatter.7.cloned.1.call-done = bf16[160,3200]{1,0:T(8,128)(2,1)} async-done(((bf16[640,3200]{1,0:T(8,128)(2,1)}), bf16[160,3200]{1,0:T(8,128)(2,1)}) %reduce-scatter.7.cloned.1.call-update) | async-done | bytes 1024016 | tf_op jit(solution)/shard_map/reduce_scatter | solution.py:38
  610.4 42.5 %reduce-scatter.9.cloned.1.call-done = bf16[160,3200]{1,0:T(8,128)(2,1)} async-done(((bf16[640,3200]{1,0:T(8,128)(2,1)}), bf16[160,3200]{1,0:T(8,128)(2,1)}) %reduce-scatter.9.cloned.1.call-update) | async-done | bytes 1024016 | tf_op jit(solution)/shard_map/reduce_scatter | solution.py:38
  652.9 132.7 %all-reduce.3.cloned.1.call-done = (bf16[1,160,3200]{2,1,0:T(8,128)(2,1)}, bf16[1,160,3200]{2,1,0:T(8,128)(2,1)}, bf16[1,160,3200]{2,1,0:T(8,128)(2,1)}, bf16[1,...) async-done(((bf16[1,160,3200]{2,1,0:T(8,128)(2,1)}, bf16[1,160,3200]{2,1,0:T(8,128)(2,1)}, bf16[1,160,3200]{2,1,0:T(8,128)(2,1)}, ...) | async-done | bytes 6144016 | tf_op jit(solution)/shard_map/psum | solution.py:38
  785.7 8.8 %fusion.45 = (bf16[2,800,640]{2,1,0:T(8,128)(2,1)}, f32[2,800,640]{2,1,0:T(8,128)}, f32[2,800,640]{2,1,0:T(8,128)}) fusion(bf16[2,800,640]{2,1,0:T(8,128)(2,1)S(1)} %copy-done.1, bf16[1,800,640]{2,1,0:T(8,128)(2,1)} %get-tuple-element.13, bf16[1,800,640]{2,1,0:T(8,128)(2,1)} %get-tuple-element.14, f32[2,800,640]{2,1,0:T(8,128)} %param.21, ...), kind=kLoop, calls=%fused_computation.76 | loop fusion | flops 19456000 | bytes 22528000 | tf_op jit(solution)/shard_map/convert_element_type | solution.py:30
  794.5 0.2 copy-done.6
  794.8 0.8 copy-done.7
  795.5 12.7 %fusion.37 = (bf16[2,160,3200]{2,1,0:T(8,128)(2,1)}, f32[2,160,3200]{2,1,0:T(8,128)}, f32[2,160,3200]{2,1,0:T(8,128)}, bf16[2,160,3200]{2,1,0:T(8,128)(2,1)}, f3...) fusion(bf16[2,160,3200]{2,1,0:T(8,128)(2,1)S(1)} %copy-done.2, bf16[1,160,3200]{2,1,0:T(8,128)(2,1)S(1)} %copy-done.4, ...), kind=kLoop, calls=%fused_computation.68 | loop fusion | flops 38912000 | bytes 45056000 | tf_op jit(solution)/shard_map/convert_element_type | solution.py:30
  (50 shorter events, 0.4 us)
Async XLA Ops:
  7.2 6.3 copy-start
  7.2 38.0 %all-gather.13.cloned.1.call-start = ((), (), s32[]{:S(2)}) async-start(), calls=%async_computation.12 | async-start | bytes 5120000 | tf_op jit(solution)/shard_map/all_gather | solution.py:35
  10.4 68.8 %all-gather.15.cloned.1.call-start = ((), (), s32[]{:S(2)}) async-start(), calls=%async_computation.13 | async-start | bytes 5120000 | tf_op jit(solution)/shard_map/all_gather | solution.py:35
  13.4 116.7 %all-gather.17.cloned.1.call-start = ((), (), s32[]{:S(2)}) async-start(), calls=%async_computation.14 | async-start | bytes 5120000 | tf_op jit(solution)/shard_map/all_gather | solution.py:35
  15.0 140.6 %all-gather.21.cloned.1.call-start = ((), (), s32[]{:S(2)}) async-start(), calls=%async_computation.16 | async-start | bytes 5120000 | tf_op jit(solution)/shard_map/all_gather | solution.py:35
  15.5 168.1 %all-gather.23.cloned.1.call-start = ((), (), s32[]{:S(2)}) async-start(), calls=%async_computation.17 | async-start | bytes 5120000 | tf_op jit(solution)/shard_map/all_gather | solution.py:35
  16.1 198.6 %all-gather.19.cloned.1.call-start = ((), (), s32[]{:S(2)}) async-start(), calls=%async_computation.15 | async-start | bytes 5120000 | tf_op jit(solution)/shard_map/all_gather | solution.py:35
  16.7 577.4 %reduce-scatter.15.cloned.1.call-start = ((), (), s32[]{:S(2)}) async-start(), calls=%async_computation.10 | async-start | bytes 5120000 | tf_op jit(solution)/shard_map/reduce_scatter | solution.py:38
  28.4 50.8 %copy-start.13 = (f32[4096]{0:T(1024)}, f32[4096]{0:T(1024)S(1)}, u32[]{:S(2)}) copy-start(f32[4096]{0:T(1024)S(1)} %add_rsqrt_fusion) | copy-start | bytes 49156
  154.9 0.6 copy-start.11
  155.5 190.2 %copy-start.8 = (f32[4096]{0:T(1024)}, f32[4096]{0:T(1024)S(1)}, u32[]{:S(2)}) copy-start(f32[4096]{0:T(1024)S(1)} %fusion.71) | copy-start | bytes 49156
  214.7 67.7 %copy-start.15 = (bf16[1,640,3200]{2,1,0:T(8,128)(2,1)S(1)}, bf16[1,640,3200]{2,1,0:T(8,128)(2,1)}, u32[]{:S(2)}) copy-start(bf16[1,640,3200]{2,1,0:T(8,128)(2,1)} %all-gather.19.cloned.1.call-done) | copy-start | bytes 12288004
  305.3 40.4 %copy-start.12 = (f32[4096]{0:T(1024)S(1)}, f32[4096]{0:T(1024)}, u32[]{:S(2)}) copy-start(f32[4096]{0:T(1024)} %copy-done.11) | copy-start | bytes 49156
  384.0 210.1 %reduce-scatter.17.cloned.1.call-start = ((), (), s32[]{:S(2)}) async-start(), calls=%async_computation.11 | async-start | bytes 5120000 | tf_op jit(solution)/shard_map/reduce_scatter | solution.py:38
  423.6 27.5 %copy-start.14 = (f32[4096]{0:T(1024)S(1)}, f32[4096]{0:T(1024)}, u32[]{:S(2)}) copy-start(f32[4096]{0:T(1024)} %copy-done.13) | copy-start | bytes 49156
  423.6 170.6 %reduce-scatter.11.cloned.1.call-start = ((), (), s32[]{:S(2)}) async-start(), calls=%async_computation.8 | async-start | bytes 5120000 | tf_op jit(solution)/shard_map/reduce_scatter | solution.py:38
  451.0 34.7 %copy-start.9 = (f32[4096]{0:T(1024)S(1)}, f32[4096]{0:T(1024)}, u32[]{:S(2)}) copy-start(f32[4096]{0:T(1024)} %copy-done.8) | copy-start | bytes 49156
  485.7 108.5 %reduce-scatter.13.cloned.1.call-start = ((), (), s32[]{:S(2)}) async-start(), calls=%async_computation.9 | async-start | bytes 5120000 | tf_op jit(solution)/shard_map/reduce_scatter | solution.py:38
  520.6 89.9 %reduce-scatter.7.cloned.1.call-start = ((), (), s32[]{:S(2)}) async-start(), calls=%async_computation.6 | async-start | bytes 5120000 | tf_op jit(solution)/shard_map/reduce_scatter | solution.py:38
  520.6 46.9 %copy-start.10 = (f32[4096]{0:T(1024)S(1)}, f32[4096]{0:T(1024)}, u32[]{:S(2)}) copy-start(f32[4096]{0:T(1024)} %copy-done.8) | copy-start | bytes 49156
  567.5 85.4 %reduce-scatter.9.cloned.1.call-start = ((), (), s32[]{:S(2)}) async-start(), calls=%async_computation.7 | async-start | bytes 5120000 | tf_op jit(solution)/shard_map/reduce_scatter | solution.py:38
  593.7 191.9 %copy-start.1 = (bf16[2,800,640]{2,1,0:T(8,128)(2,1)S(1)}, bf16[2,800,640]{2,1,0:T(8,128)(2,1)}, u32[]{:S(2)}) copy-start(bf16[2,800,640]{2,1,0:T(8,128)(2,1)} %param.15) | copy-start | bytes 6144004
  593.7 191.9 %all-reduce.3.cloned.1.call-start = ((), (), s32[]{:S(2)}) async-start(), calls=%async_computation.18 | async-start | bytes 12288000 | tf_op jit(solution)/shard_map/psum | solution.py:38
  785.6 8.9 %copy-start.2 = (bf16[2,160,3200]{2,1,0:T(8,128)(2,1)S(1)}, bf16[2,160,3200]{2,1,0:T(8,128)(2,1)}, u32[]{:S(2)}) copy-start(bf16[2,160,3200]{2,1,0:T(8,128)(2,1)} %param.13) | copy-start | bytes 6144004
  785.6 8.9 %copy-start.3 = (bf16[2,160,3200]{2,1,0:T(8,128)(2,1)S(1)}, bf16[2,160,3200]{2,1,0:T(8,128)(2,1)}, u32[]{:S(2)}) copy-start(bf16[2,160,3200]{2,1,0:T(8,128)(2,1)} %param.14) | copy-start | bytes 6144004
  785.6 8.9 %copy-start.4 = (bf16[1,160,3200]{2,1,0:T(8,128)(2,1)S(1)}, bf16[1,160,3200]{2,1,0:T(8,128)(2,1)}, u32[]{:S(2)}) copy-start(bf16[1,160,3200]{2,1,0:T(8,128)(2,1)} %get-tuple-element.9) | copy-start | bytes 3072004
  785.6 8.9 %copy-start.5 = (bf16[1,160,3200]{2,1,0:T(8,128)(2,1)S(1)}, bf16[1,160,3200]{2,1,0:T(8,128)(2,1)}, u32[]{:S(2)}) copy-start(bf16[1,160,3200]{2,1,0:T(8,128)(2,1)} %get-tuple-element.10) | copy-start | bytes 3072004
  785.6 9.1 %copy-start.6 = (bf16[1,160,3200]{2,1,0:T(8,128)(2,1)S(1)}, bf16[1,160,3200]{2,1,0:T(8,128)(2,1)}, u32[]{:S(2)}) copy-start(bf16[1,160,3200]{2,1,0:T(8,128)(2,1)} %get-tuple-element.11) | copy-start | bytes 3072004
  785.6 9.9 %copy-start.7 = (bf16[1,160,3200]{2,1,0:T(8,128)(2,1)S(1)}, bf16[1,160,3200]{2,1,0:T(8,128)(2,1)}, u32[]{:S(2)}) copy-start(bf16[1,160,3200]{2,1,0:T(8,128)(2,1)} %get-tuple-element.12) | copy-start | bytes 3072004
Sparse Core Ops, SparseCore 0:
  10.5 34.6 all-gather.12
  47.3 31.8 all-gather.14
  81.3 31.8 all-gather.16
  115.1 31.8 all-gather.20
  149.0 31.8 all-gather.22
  182.8 31.8 all-gather.18
  384.2 39.4 reduce-scatter.14
  426.8 39.4 reduce-scatter.16
  485.8 39.4 reduce-scatter.10
  528.3 39.4 reduce-scatter.12
  570.9 39.4 reduce-scatter.6
  613.4 39.4 reduce-scatter.8
  657.6 127.9 all-reduce.2
where the time goes:
time: 824 us; the launch traced here: 815 us
  matrix products  529 us (64%)
  waiting for transfers between devices  208 us (25%)
  other arithmetic  37 us (4%)
  local copies, waits for them, and re-layouts  25.1 us (3%)
  between operations  14.6 us (2%)
    dot_general x5, matrix products, layer(): gate = jnp.dot(a, w['w_gate'], preferred_element_type=jnp.float32)  193 us
    dot_general x5, matrix products, layer(): up = jnp.dot(a, w['w_up'], preferred_element_type=jnp.float32)  190 us
    dot_general x5, matrix products, matmul(): jnp.dot(a, w, preferred_element_type=jnp.float32).astype(jnp.bfloat16)  146 us
    psum x1, waiting for transfers between devices, summed(): lax.psum(lax.psum_scatter(term, 's', scatter_dimension=0, tiled=True), 'r')  133 us
    reduce_scatter x6, waiting for transfers between devices, summed(): lax.psum_scatter(term, 's', scatter_dimension=0, tiled=True)  58.8 us
    convert_element_type x2, other arithmetic, adamw(): return ((w - 0.02 * step).astype(jnp.bfloat16), m, v)  21.5 us
    unnamed x34, local copies, waits for them, and re-layouts  17.6 us
  transfers between devices with their start and end apart: 13, of which 6 were waited for; matrix products, arithmetic and copies ran while one was open for 49% of the time, Pallas kernels for 0%

commit v1 on v0

v1 whole, which is shorter than its diff:
```python
import functools

import jax
import jax.numpy as jnp
from jax import lax
from jax.experimental import pallas as pl
from jax.experimental.pallas import tpu as pltpu
from jax.sharding import PartitionSpec as P

MESH = pl.DeviceIdType.MESH
F32, BF16 = jnp.float32, jnp.bfloat16
VMEM_LIMIT = 67043328


def dot(a, b, over_a, over_b):
    return lax.dot_general(a, b, (((over_a,), (over_b,)), ((), ())), preferred_element_type=F32)


def sigmoid(g):
    return 0.5 * jnp.tanh(0.5 * g) + 0.5


def scale_of(wide):
    return lax.rsqrt(jnp.mean(wide * wide, -1, keepdims=True) + 1e-6)


def places():
    s, r = lax.axis_index("s"), lax.axis_index("r")
    other = s + 1 - 2 * lax.rem(s, 2)
    return s, r, other, lax.rem(s + 2, 4), lax.rem(r + 2, 4), r + 1 - 2 * lax.rem(r, 2)


def remote(src, dst, send, recv, **where):
    return pltpu.make_async_remote_copy(src_ref=src, dst_ref=dst, send_sem=send, recv_sem=recv, device_id=where, device_id_type=MESH)


def greet(*peers):
    barrier = pltpu.get_barrier_semaphore()
    for peer in peers:
        pl.semaphore_signal(barrier, inc=1, device_id=peer, device_id_type=MESH)
    pl.semaphore_wait(barrier, len(peers))


def forward_kernel(sizes, x_ref, wg_ref, wu_ref, wd_ref, h_ref, w_gu, w_d, a_s, hid_s, gu_s, d_s, own_sem, out_sem, x_send, x_recv, y_send, y_recv, c_send, c_recv):
    tokens, d, ff, chunk, chunks, block = sizes
    steps = tokens // block
    c, t = pl.program_id(0), pl.program_id(1)
    s, r, other, across, by_y, _ = places()
    y = lax.div(r, 2)
    rows_gu, rows_d = d // 4, ff // 4
    pieces = 2 * chunks + 2
    first_1 = chunks + 2

    def parts(p, holder, half):
        n_gu, n_d = rows_gu // 2, rows_d // 2
        at_gu = pl.ds(pl.multiple_of(holder * rows_gu + half * n_gu, 16), n_gu)
        at_d = pl.ds(pl.multiple_of(holder * rows_d + half * n_d, 16), n_d)
        if p < chunks:
            return [gu_s.at[p, at_gu]]
        if p == chunks:
            return [d_s.at[at_d]]
        if p == chunks + 1:
            return [w_d.at[0, at_d]]
        return [w_gu.at[p - first_1, at_gu]]

    def own(p, half):
        n_gu, n_d = rows_gu // 2, rows_d // 2
        at_gu = pl.ds(pl.multiple_of(half * n_gu, 16), n_gu)
        at_d = pl.ds(pl.multiple_of(half * n_d, 16), n_d)
        to = parts(p, s, half)[0]
        if p in (chunks, chunks + 1):
            return [(wd_ref.at[p - chunks, at_d], to)]
        layer, n = (0, p) if p < chunks else (1, p - first_1)
        cols = pl.ds(n * chunk, chunk)
        return [(wg_ref.at[layer, at_gu, cols], to.at[:, pl.ds(0, chunk)]), (wu_ref.at[layer, at_gu, cols], to.at[:, pl.ds(chunk, chunk)])]

    def own_whole(p):
        at_gu = pl.ds(pl.multiple_of(s * rows_gu, 16), rows_gu)
        at_d = pl.ds(pl.multiple_of(s * rows_d, 16), rows_d)
        if p in (chunks, chunks + 1):
            return [(wd_ref.at[p - chunks], (d_s if p == chunks else w_d.at[0]).at[at_d])]
        layer, n = (0, p) if p < chunks else (1, p - first_1)
        to = (gu_s.at[p] if p < chunks else w_gu.at[p - first_1]).at[at_gu]
        cols = pl.ds(n * chunk, chunk)
        return [(wg_ref.at[layer, :, cols], to.at[:, pl.ds(0, chunk)]), (wu_ref.at[layer, :, cols], to.at[:, pl.ds(chunk, chunk)])]

    def own_copies(p):
        return [pltpu.make_async_copy(a, b, own_sem.at[p, i]) for i, (a, b) in enumerate(own_whole(p))]

    def x_copies(p):
        return [remote(a, b, x_send.at[p, i], x_recv.at[p, i], s=across) for i, (a, b) in enumerate(own(p, y))]

    def own_to_core(p):
        return [remote(a, b, c_send.at[p, i], c_recv.at[p, i], s=other) for i, (a, b) in enumerate(own_whole(p))]

    def y_copy(p):
        ref = parts(p, across, y)[0]
        return remote(ref, ref, y_send.at[p], y_recv.at[p], r=by_y)

    def to_core(p, half, i):
        ref = parts(p, across, half)[0]
        return remote(ref, ref, c_send.at[p, 2 + i], c_recv.at[p, 2 + i], s=other)

    def out_copy(p):
        if p < chunks:
            return pltpu.make_async_copy(gu_s.at[p], w_gu.at[chunks + p], out_sem.at[p])
        return pltpu.make_async_copy(d_s, w_d.at[1], out_sem.at[p])

    def x_done(p):
        for copy in x_copies(p):
            copy.wait()
        y_copy(p).start()
        to_core(p, y, 0).start()

    def y_done(p):
        y_copy(p).wait()
        to_core(p, 1 - y, 1).start()

    def ready(p):
        for copy in own_copies(p) + own_to_core(p) + [to_core(p, y, 0), to_core(p, 1 - y, 1)]:
            copy.wait()
        if p <= chunks:
            out_copy(p).start()

    def at(cc, tt, do, *pieces_of):
        @pl.when((c == cc) & (t == tt))
        def _():
            for p in pieces_of:
                do(p)

    @pl.when((c == 0) & (t == 0))
    def _():
        greet({"s": other}, {"s": across}, {"r": by_y})
        for p in range(pieces):
            for copy in x_copies(p) + own_to_core(p) + own_copies(p):
                copy.start()

    @pl.when(c == 0)
    def _():
        wide = x_ref[...].astype(F32)
        a_s[pl.ds(pl.multiple_of(t * block, block), block)] = (wide * scale_of(wide)).astype(BF16)

    at(0, 0, x_done, 0)
    at(0, 0, y_done, 0)
    for n in range(chunks):
        at(n, 0, ready, n)
        if n + 1 < chunks:
            at(n, 1, x_done, n + 1)
            at(n, 3, y_done, n + 1)
    at(chunks - 1, 0, x_done, chunks)
    at(chunks - 1, 3, y_done, chunks)
    at(chunks - 1, 3, x_done, chunks + 1)
    at(chunks, 0, ready, chunks)
    at(chunks, 0, y_done, chunks + 1)
    at(chunks, 0, x_done, chunks + 2)
    at(chunks, 1, y_done, chunks + 2)
    at(chunks, 1, x_done, chunks + 3)
    at(chunks, 2, y_done, chunks + 3)
    at(chunks, 2, x_done, chunks + 4, chunks + 5)
    at(chunks, 3, y_done, chunks + 4, chunks + 5)
    at(chunks, 3, x_done, chunks + 6)

    rows = pl.ds(pl.multiple_of(t * block, block), block)

    @pl.when(c < chunks)
    def _():
        gu = dot(a_s[rows], gu_s[c], 1, 0)
        g, u = gu[:, :chunk], gu[:, chunk:]
        hid_s[rows, pl.ds(pl.multiple_of(c * chunk, 128), chunk)] = (g * sigmoid(g) * u).astype(BF16)

    @pl.when(c == chunks)
    def _():
        added = dot(hid_s[rows], d_s[...], 1, 0).astype(BF16)
        h_ref[...] = (x_ref[...].astype(F32) + added.astype(F32)).astype(BF16)

    at(chunks, steps - 1, y_done, chunks + 6)
    at(chunks, steps - 1, ready, *range(chunks + 1, pieces))

    @pl.when((c == chunks) & (t == steps - 1))
    def _():
        for p in range(chunks + 1):
            out_copy(p).wait()


def forward(x, wg, wu, wd, chunk, block):
    (tokens, d), ff = x.shape, wg.shape[-1]
    chunks = ff // chunk
    pieces = 2 * chunks + 2
    sizes = (tokens, d, ff, chunk, chunks, block)
    whole = lambda a: pl.BlockSpec(a.shape, lambda c, t: (0,) * a.ndim, pipeline_mode=pl.Buffered(1))
    dma = pltpu.SemaphoreType.DMA
    return pl.pallas_call(
        functools.partial(forward_kernel, sizes),
        grid=(chunks + 1, tokens // block),
        in_specs=[pl.BlockSpec((block, d), lambda c, t: (jnp.where((c == 0) | (c == chunks), t, 0), 0)), whole(wg), whole(wu), whole(wd)],
        out_specs=[
            pl.BlockSpec((block, d), lambda c, t: (jnp.where(c == chunks, t, 0), 0)),
            pl.BlockSpec(memory_space=pl.ANY),
            pl.BlockSpec(memory_space=pl.ANY),
        ],
        out_shape=[
            jax.ShapeDtypeStruct((tokens, d), BF16),
            jax.ShapeDtypeStruct((2 * chunks, d, 2 * chunk), BF16),
            jax.ShapeDtypeStruct((2, ff, d), BF16),
        ],
        scratch_shapes=[
            pltpu.VMEM((tokens, d), BF16),
            pltpu.VMEM((tokens, ff), BF16),
            pltpu.VMEM((chunks, d, 2 * chunk), BF16),
            pltpu.VMEM((ff, d), BF16),
            dma((pieces, 2)),
            dma((chunks + 1,)),
            dma((pieces, 2)),
            dma((pieces, 2)),
            dma((pieces,)),
            dma((pieces,)),
            dma((pieces, 4)),
            dma((pieces, 4)),
        ],
        compiler_params=pltpu.CompilerParams(collective_id=0, has_side_effects=True, vmem_limit_bytes=VMEM_LIMIT),
        name="forward",
    )(x, wg, wu, wd)


def backward_kernel(sizes, h_ref, dy_ref, x_ref, wgu_ref, wd_ref, gg, gu, gd, a_s, dy_s, da_s, acc_s, mine, c_out, c_in, x_out, x_in, y_out, y_in, z_out, z_in, done,
                    c_sem, x_sem, y_sem, z_sem, d_send, d_recv, l_sem):
    tokens, d, ff, chunk, chunks, block, sub = sizes
    last, steps = 2 * chunks - 1, tokens // block
    c, t = pl.program_id(0), pl.program_id(1)
    s, r, other, across, by_y, by_z = places()
    x, core = lax.div(s, 2), lax.rem(s, 2)
    n = d // 4
    rows = pl.ds(pl.multiple_of(t * block, block), block)

    def to_core(k):
        return remote(c_out, c_in.at[lax.rem(k, 2)], c_sem.at[0], c_sem.at[1 + lax.rem(k, 2)], s=other)

    def to_x(k):
        return remote(x_out, x_in.at[lax.rem(k, 2)], x_sem.at[0], x_sem.at[1 + lax.rem(k, 2)], s=across)

    def to_y(k):
        return remote(y_out, y_in.at[lax.rem(k, 2)], y_sem.at[0], y_sem.at[1 + lax.rem(k, 2)], r=by_y)

    def to_z(k):
        return remote(z_out, z_in.at[lax.rem(k, 2)], z_sem.at[0], z_sem.at[1 + lax.rem(k, 2)], r=by_z)

    def finals(k):
        layer, of = 1 - lax.div(k, chunks), lax.rem(k, chunks)
        cols = pl.ds(pl.multiple_of(of * chunk, 128), chunk)
        number = 4 * of + s
        owner, place = lax.div(number, chunks), lax.rem(number, chunks)
        to = gd.at[layer, pl.ds(pl.multiple_of(place * n, 16), n)]
        down = done.at[:, pl.ds(2 * chunk, d)]
        here = [
            pltpu.make_async_copy(done.at[:, pl.ds(0, chunk)], gg.at[layer, :, cols], l_sem.at[0]),
            pltpu.make_async_copy(done.at[:, pl.ds(chunk, chunk)], gu.at[layer, :, cols], l_sem.at[1]),
        ]
        return here, owner == s, pltpu.make_async_copy(down, to, l_sem.at[2]), remote(down, to, d_send, d_recv.at[layer, place], s=owner)

    def start_finals(k):
        here, stays, local, away = finals(k)
        for copy in here:
            copy.start()
        pl.when(stays)(local.start)
        pl.when(jnp.logical_not(stays))(away.start)

    def end_finals(k):
        here, stays, local, away = finals(k)
        for copy in here:
            copy.wait()
        pl.when(stays)(local.wait)
        pl.when(jnp.logical_not(stays))(away.wait_send)

    @pl.when((c == 0) & (t == 0))
    def _():
        greet({"s": other}, {"s": across}, {"s": 3 - s}, {"r": by_y}, {"r": by_z})

    @pl.when((t == 1) & (c >= 2))
    def _():
        k = c - 2
        to_y(k).wait()
        z_out[...] = (y_out[...].astype(F32) + y_in[lax.rem(k, 2)].astype(F32)).astype(BF16)
        to_z(k).start()

    @pl.when((t == 1) & (c >= 1) & (c <= last + 1))
    def _():
        k = c - 1
        to_core(k).wait()
        x_out[...] = (mine[1 - x] + c_in[lax.rem(k, 2), 1 - x].astype(F32)).astype(BF16)
        to_x(k).start()
        mine[x] += c_in[lax.rem(k, 2), x].astype(F32)

    @pl.when((t == 3) & (c >= 2))
    def _():
        k = c - 2
        to_z(k).wait()
        pl.when(k >= 1)(lambda: end_finals(k - 1))
        done[...] = (z_out[...].astype(F32) + z_in[lax.rem(k, 2)].astype(F32)).astype(BF16)
        start_finals(k)

    @pl.when((t == 3) & (c >= 1) & (c <= last + 1))
    def _():
        k = c - 1
        to_x(k).wait()
        y_out[...] = (mine[x] + x_in[lax.rem(k, 2)].astype(F32)).astype(BF16)
        to_y(k).start()

    @pl.when(c == 0)
    def _():
        wide = h_ref[...].astype(F32)
        a_s[rows] = (wide * scale_of(wide)).astype(BF16)
        dy_s[rows] = dy_ref[...]
        da_s[rows] = jnp.zeros((block, d), F32)

    @pl.when(c == chunks)
    def _():
        wide = x_ref[...].astype(F32)
        a_s[rows] = (wide * scale_of(wide)).astype(BF16)

    @pl.when(c <= last)
    def _():
        @pl.when(t == 0)
        def _():
            acc_s[...] = jnp.zeros_like(acc_s)

        for i in range(block // sub):
            at = pl.ds(pl.multiple_of(t * block + i * sub, sub), sub)
            a, dy = a_s[at], dy_s[at]
            both = dot(a, wgu_ref[0], 1, 0)
            dh = dot(dy, wd_ref[0], 1, 1).astype(BF16).astype(F32)
            g, u = both[:, :chunk], both[:, chunk:]
            sg = sigmoid(g)
            sl = g * sg
            hid = (sl * u).astype(BF16)
            by_u = (dh * sl).astype(BF16)
            by_g = (dh * u * (sg * (1 + g * (1 - sg)))).astype(BF16)
            by_gu = jnp.concatenate([by_g, by_u], 1)
            acc_s[:, : 2 * chunk] += dot(a, by_gu, 0, 0)
            acc_s[:, 2 * chunk :] += dot(hid, dy, 0, 0)

            @pl.when(c < chunks)
            def _():
                da_s[at] += dot(by_gu, wgu_ref[0], 1, 1)

        @pl.when(c == chunks - 1)
        def _():
            da = da_s[rows].astype(BF16).astype(F32)
            wide = h_ref[...].astype(F32)
            scale = scale_of(wide)
            along = jnp.sum(da * wide, -1, keepdims=True) * (scale * scale * scale) * (1.0 / d)
            dy_s[rows] = (dy_s[rows].astype(F32) + (da * scale - wide * along).astype(BF16).astype(F32)).astype(BF16)

        @pl.when(t == steps - 1)
        def _():
            for i in range(2):
                mine[i] = acc_s[pl.ds(pl.multiple_of((2 * i + core) * n, 8), n)]
                c_out[i] = acc_s[pl.ds(pl.multiple_of((2 * i + 1 - core) * n, 8), n)].astype(BF16)
            to_core(c).start()

    @pl.when((c == last + 2) & (t == steps - 1))
    def _():
        end_finals(last)
        for layer in range(2):
            for place in range(chunks):
                number = s * chunks + place
                to = gd.at[layer, pl.ds(place * n, n)]
                from_other = lax.rem(number, 4) != s
                copy = remote(done.at[:, pl.ds(2 * chunk, d)], to, d_send, d_recv.at[layer, place], s=other)
                pl.when(from_other)(copy.wait_recv)


def backward(h, dy, x, wgu, wd, chunk, block, sub):
    (tokens, d), ff = x.shape, wd.shape[1]
    chunks = ff // chunk
    n, last = d // 4, 2 * chunks - 1
    sizes = (tokens, d, ff, chunk, chunks, block, sub)
    dma = pltpu.SemaphoreType.DMA
    wide = 2 * chunk + d
    at = lambda *when: pl.BlockSpec((block, d), lambda c, t: (jnp.where(functools.reduce(jnp.logical_or, [c == w for w in when]), t, 0), 0))
    return pl.pallas_call(
        functools.partial(backward_kernel, sizes),
        grid=(last + 3, tokens // block),
        in_specs=[
            at(0, chunks - 1),
            at(0),
            at(chunks),
            pl.BlockSpec((1, d, 2 * chunk), lambda c, t: (jnp.minimum(c, last), 0, 0)),
            pl.BlockSpec((1, chunk, d), lambda c, t: (lax.div(jnp.minimum(c, last), chunks), lax.rem(jnp.minimum(c, last), chunks), 0)),
        ],
        out_specs=[pl.BlockSpec(memory_space=pl.ANY)] * 3,
        out_shape=[
            jax.ShapeDtypeStruct((2, n, ff), BF16),
            jax.ShapeDtypeStruct((2, n, ff), BF16),
            jax.ShapeDtypeStruct((2, ff // 4, d), BF16),
        ],
        scratch_shapes=[
            pltpu.VMEM((tokens, d), BF16),
            pltpu.VMEM((tokens, d), BF16),
            pltpu.VMEM((tokens, d), F32),
            pltpu.VMEM((d, wide), F32),
            pltpu.VMEM((2, n, wide), F32),
            pltpu.VMEM((2, n, wide), BF16),
            pltpu.VMEM((2, 2, n, wide), BF16),
            pltpu.VMEM((n, wide), BF16),
            pltpu.VMEM((2, n, wide), BF16),
            pltpu.VMEM((n, wide), BF16),
            pltpu.VMEM((2, n, wide), BF16),
            pltpu.VMEM((n, wide), BF16),
            pltpu.VMEM((2, n, wide), BF16),
            pltpu.VMEM((n, wide), BF16),
            dma((3,)),
            dma((3,)),
            dma((3,)),
            dma((3,)),
            dma,
            dma((2, chunks)),
            dma((3,)),
        ],
        compiler_params=pltpu.CompilerParams(collective_id=1, has_side_effects=True, vmem_limit_bytes=VMEM_LIMIT),
        name="backward",
    )(h, dy, x, wgu, wd)


def adamw(w, m, v, g):
    m = 0.9 * m + 0.1 * g
    v = 0.95 * v + 0.05 * g * g
    step = m * lax.rsqrt(v + 1e-8) + 0.1 * w
    return (w - 0.02 * step).astype(BF16), m, v


def solution(mesh):
    def step(x, dy, *arrays):
        weights, m, v = (arrays[i : i + 3] for i in (0, 3, 6))
        x, dy = x[0], dy[0]
        h, wgu, wd = forward(x, *weights, 640, 1024)
        gradients = backward(h, dy, x, wgu, wd, 640, 1024, 512)
        new = [adamw(w.astype(F32), m, v, g.astype(F32)) for w, m, v, g in zip(weights, m, v, gradients, strict=True)]
        return tuple(one[which] for which in range(3) for one in new)

    states, cut = P(("rep", "r", "s"), None, None), P(None, "s", None)
    return jax.shard_map(
        step,
        mesh=mesh,
        in_specs=(states, states) + (cut,) * 9,
        out_specs=(P("rep", "s", None),) * 9,
        check_vma=False,
    )
```

time: 824 us -> 539 us (0.65); the launches traced: 815 us -> 539 us
  matrix products: 529 us -> 0 us
  Pallas kernels: 0 us -> 515 us
  waiting for transfers between devices: 208 us -> 0 us
  local copies, waits for them, and re-layouts: 25.1 us -> 2.37 us
  other arithmetic: 37 us -> 20.6 us
  between operations: 14.6 us -> 0.69 us
    dot_general x15 -> x0, matrix products: 529 us -> none  [the longest x5 193 us: layer(): gate = jnp.dot(a, w['w_gate'], preferred_element_type=jnp.float32)]
    pallas_call x0 -> x2, Pallas kernels: none -> 515 us  [the longest x1 394 us: backward(): pl.pallas_call(functools.partial(backward_kernel, sizes), grid=(last + 3,...]
    psum x1 -> x0, waiting for transfers between devices: 133 us -> none  [summed(): lax.psum(lax.psum_scatter(term, 's', scatter_dimension=0, tiled=True), 'r')]
    reduce_scatter x6 -> x0, waiting for transfers between devices: 58.8 us -> none  [summed(): lax.psum_scatter(term, 's', scatter_dimension=0, tiled=True)]
    unnamed x34 -> x8, local copies, waits for them, and re-layouts: 17.6 us -> 2.37 us
    all_gather x6 -> x0, waiting for transfers between devices: 15.2 us -> none  [fetched(): lax.all_gather(w[number], 's', axis=0, tiled=True)]
    add_any x1 -> x0, other arithmetic: 11.9 us -> none  [normed(): wide = h.astype(jnp.float32)]
  transfers between devices with their start and end apart: 13 -> 0, of which waited for: 6 -> 0; matrix products, arithmetic and copies ran while one was open for 49% -> 0% of each run, Pallas kernels for 0% -> 0%
where the time goes in v1:
time: 539 us
  Pallas kernels  515 us (96%)
  other arithmetic  20.6 us (4%)
    pallas_call x1, Pallas kernels, backward(): pl.pallas_call(functools.partial(backward_kernel, sizes), grid=(last + 3,...  394 us
    pallas_call x1, Pallas kernels, forward(): pl.pallas_call(functools.partial(forward_kernel, sizes), grid=(chunks + 1...  122 us
    convert_element_type x2, other arithmetic, adamw(): return ((w - 0.02 * step).astype(BF16), m, v)  20.6 us

profile of v1, /device:TPU:0, one launch (start us, length us, event | category | flops | bytes accessed | tf_op | source)
XLA Modules:
  0.0 538.9 jit_solution(7671227609492754105)
XLA Ops:
  0.6 121.7 %forward.1 = (bf16[4096,640]{1,0:T(8,128)(2,1)}, bf16[10,640,1280]{2,1,0:T(8,128)(2,1)}, bf16[2,3200,640]{2,1,0:T(8,128)(2,1)}) custom-call(bf16[4096,640]{1,0:T(8,128)(2,1)} %bitcast.2, bf16[2,160,3200]{2,1,0:T(8,128)(2,1)} %wg_ref.1, bf16[2,160,3200]{2,1,0:T(8,128)(2,1)} %wu_ref.1, bf16[2,800,640]{2,1,0:T(8,128)(2,1)} %wd_ref.1), custom_call_target="tpu_custom_call" | custom-call | tf_op jit(solution)/shard_map/forward/pallas_call | solution.py:192
  122.3 393.5 %backward.1 = (bf16[2,160,3200]{2,1,0:T(8,128)(2,1)}, bf16[2,160,3200]{2,1,0:T(8,128)(2,1)}, bf16[2,800,640]{2,1,0:T(8,128)(2,1)}) custom-call(bf16[4096,640]{1,0:T(8,128)(2,1)} %get-tuple-element.15.h_ref, bf16[4096,640]{1,0:T(8,128)(2,1)} %bitcast.4, bf16[4096,640]{1,0:T(8,128)(2,1)} %bitcast.3, bf16[10,640,1280]{2,1,0:T(8,128)(2,1)} %get-tuple-element.16.wgu_ref, ...), custom_call_target="tpu_custom_call" | custom-call | tf_op jit(solution)/shard_map/backward/pallas_call | solution.py:380
  515.8 0.0 copy-start
  515.9 0.0 copy-start.1
  515.9 0.0 copy-start.2
  515.9 0.0 copy-start.3
  515.9 8.9 %fusion.10 = (bf16[2,800,640]{2,1,0:T(8,128)(2,1)}, f32[2,800,640]{2,1,0:T(8,128)}, f32[2,800,640]{2,1,0:T(8,128)}) fusion(bf16[2,800,640]{2,1,0:T(8,128)(2,1)} %wd_ref.1, bf16[2,800,640]{2,1,0:T(8,128)(2,1)} %get-tuple-element.20, f32[2,800,640]{2,1,0:T(8,128)} %param.21, f32[2,800,640]{2,1,0:T(8,128)} %param.18), kind=kLoop, calls=%fused_computation.22 | loop fusion | flops 16384000 | bytes 22528000 | tf_op jit(solution)/shard_map/convert_element_type | solution.py:428
  524.8 0.0 copy-done
  524.8 0.0 copy-done.1
  524.8 1.8 copy-done.2
  526.5 0.6 copy-done.3
  527.1 11.7 %fusion.2 = (bf16[2,160,3200]{2,1,0:T(8,128)(2,1)}, f32[2,160,3200]{2,1,0:T(8,128)}, f32[2,160,3200]{2,1,0:T(8,128)}, bf16[2,160,3200]{2,1,0:T(8,128)(2,1)}, f32...) fusion(bf16[2,160,3200]{2,1,0:T(8,128)(2,1)S(1)} %copy-done, bf16[2,160,3200]{2,1,0:T(8,128)(2,1)S(1)} %copy-done.3, ...), kind=kLoop, calls=%fused_computation.14 | loop fusion | flops 32768000 | bytes 45056000 | tf_op jit(solution)/shard_map/convert_element_type | solution.py:428
Async XLA Ops:
  515.8 8.9 %copy-start = (bf16[2,160,3200]{2,1,0:T(8,128)(2,1)S(1)}, bf16[2,160,3200]{2,1,0:T(8,128)(2,1)}, u32[]{:S(2)}) copy-start(bf16[2,160,3200]{2,1,0:T(8,128)(2,1)} %wg_ref.1) | copy-start | bytes 6144004
  515.9 8.9 %copy-start.1 = (bf16[2,160,3200]{2,1,0:T(8,128)(2,1)S(1)}, bf16[2,160,3200]{2,1,0:T(8,128)(2,1)}, u32[]{:S(2)}) copy-start(bf16[2,160,3200]{2,1,0:T(8,128)(2,1)} %wu_ref.1) | copy-start | bytes 6144004
  515.9 10.7 %copy-start.2 = (f32[2,160,3200]{2,1,0:T(8,128)S(1)}, f32[2,160,3200]{2,1,0:T(8,128)}, u32[]{:S(2)}) copy-start(f32[2,160,3200]{2,1,0:T(8,128)} %param.19) | copy-start | bytes 12288004
  515.9 11.2 %copy-start.3 = (bf16[2,160,3200]{2,1,0:T(8,128)(2,1)S(1)}, bf16[2,160,3200]{2,1,0:T(8,128)(2,1)}, u32[]{:S(2)}) copy-start(bf16[2,160,3200]{2,1,0:T(8,128)(2,1)} %get-tuple-element.18) | copy-start | bytes 6144004

commit v2 on v1

--- a/solution.py
+++ b/solution.py
@@ -42,7 +42,7 @@
 
 
 def forward_kernel(sizes, x_ref, wg_ref, wu_ref, wd_ref, h_ref, w_gu, w_d, a_s, hid_s, gu_s, d_s, own_sem, out_sem, x_send, x_recv, y_send, y_recv, c_send, c_recv):
-    tokens, d, ff, chunk, chunks, block = sizes
+    tokens, d, ff, chunk, chunks, block, sub = sizes
     steps = tokens // block
     c, t = pl.program_id(0), pl.program_id(1)
     s, r, other, across, by_y, _ = places()
@@ -140,40 +140,33 @@
         wide = x_ref[...].astype(F32)
         a_s[pl.ds(pl.multiple_of(t * block, block), block)] = (wide * scale_of(wide)).astype(BF16)
 
-    at(0, 0, x_done, 0)
-    at(0, 0, y_done, 0)
-    for n in range(chunks):
-        at(n, 0, ready, n)
-        if n + 1 < chunks:
-            at(n, 1, x_done, n + 1)
-            at(n, 3, y_done, n + 1)
-    at(chunks - 1, 0, x_done, chunks)
-    at(chunks - 1, 3, y_done, chunks)
-    at(chunks - 1, 3, x_done, chunks + 1)
-    at(chunks, 0, ready, chunks)
-    at(chunks, 0, y_done, chunks + 1)
-    at(chunks, 0, x_done, chunks + 2)
-    at(chunks, 1, y_done, chunks + 2)
-    at(chunks, 1, x_done, chunks + 3)
-    at(chunks, 2, y_done, chunks + 3)
-    at(chunks, 2, x_done, chunks + 4, chunks + 5)
-    at(chunks, 3, y_done, chunks + 4, chunks + 5)
-    at(chunks, 3, x_done, chunks + 6)
+    last = chunks - 1
+    for cc, tt, do, p in (
+        (0, 0, x_done, 0), (0, 0, x_done, 1), (0, 0, y_done, 0), (0, 0, ready, 0), (0, 1, x_done, 2), (0, 2, y_done, 1), (0, 2, x_done, 3), (0, 3, x_done, 4),
+        (1, 0, ready, 1), (1, 0, y_done, 2), (1, 1, y_done, 3), (1, 3, y_done, 4), (1, 3, x_done, 5), (2, 0, ready, 2),
+        (3, 0, ready, 3), (3, 0, y_done, 5), (3, 0, x_done, 6), (3, 1, x_done, 7), (3, 2, x_done, 8), (4, 0, ready, 4), (4, 0, x_done, 9), (4, 1, y_done, 6),
+        (4, 1, x_done, 10), (4, 3, y_done, 7), (4, 3, x_done, 11), (5, 0, ready, 5), (5, 0, y_done, 8), (5, 1, y_done, 9), (5, 2, y_done, 10), (5, 3, y_done, 11),
+    ):
+        at(cc, tt, do, p)
 
     rows = pl.ds(pl.multiple_of(t * block, block), block)
 
     @pl.when(c < chunks)
     def _():
-        gu = dot(a_s[rows], gu_s[c], 1, 0)
-        g, u = gu[:, :chunk], gu[:, chunk:]
-        hid_s[rows, pl.ds(pl.multiple_of(c * chunk, 128), chunk)] = (g * sigmoid(g) * u).astype(BF16)
+        for i in range(block // sub):
+            at_i = pl.ds(pl.multiple_of(t * block + i * sub, sub), sub)
+            a = a_s[at_i]
+            for j in range(chunk // 128):
+                gate, up = pl.ds(j * 128, 128), pl.ds(chunk + j * 128, 128)
+                both = dot(a, jnp.concatenate([gu_s[c, :, gate], gu_s[c, :, up]], 1), 1, 0)
+                g, u = both[:, :128], both[:, 128:]
+                hid_s[at_i, pl.ds(pl.multiple_of(c * chunk + j * 128, 128), 128)] = (g * sigmoid(g) * u).astype(BF16)
 
     @pl.when(c == chunks)
     def _():
         added = dot(hid_s[rows], d_s[...], 1, 0).astype(BF16)
         h_ref[...] = (x_ref[...].astype(F32) + added.astype(F32)).astype(BF16)
 
-    at(chunks, steps - 1, y_done, chunks + 6)
     at(chunks, steps - 1, ready, *range(chunks + 1, pieces))
 
     @pl.when((c == chunks) & (t == steps - 1))
@@ -182,11 +175,11 @@
             out_copy(p).wait()
 
 
-def forward(x, wg, wu, wd, chunk, block):
+def forward(x, wg, wu, wd, chunk, block, sub):
     (tokens, d), ff = x.shape, wg.shape[-1]
     chunks = ff // chunk
     pieces = 2 * chunks + 2
-    sizes = (tokens, d, ff, chunk, chunks, block)
+    sizes = (tokens, d, ff, chunk, chunks, block, sub)
     whole = lambda a: pl.BlockSpec(a.shape, lambda c, t: (0,) * a.ndim, pipeline_mode=pl.Buffered(1))
     dma = pltpu.SemaphoreType.DMA
     return pl.pallas_call(
@@ -222,8 +215,8 @@
     )(x, wg, wu, wd)
 
 
-def backward_kernel(sizes, h_ref, dy_ref, x_ref, wgu_ref, wd_ref, gg, gu, gd, a_s, dy_s, da_s, acc_s, mine, c_out, c_in, x_out, x_in, y_out, y_in, z_out, z_in, done,
-                    c_sem, x_sem, y_sem, z_sem, d_send, d_recv, l_sem):
+def backward_kernel(sizes, h_ref, dy_ref, x_ref, wgu_ref, wd_ref, gg, gu, gd, a_s, dy_s, da_s, acc_s, mine, c_out, c_in, x_in, y_out, y_in, z_out, z_in,
+                    c_sem, x_sem, y_sem, z_sem, d_send, d_recv, l_sem, r_sem):
     tokens, d, ff, chunk, chunks, block, sub = sizes
     last, steps = 2 * chunks - 1, tokens // block
     c, t = pl.program_id(0), pl.program_id(1)
@@ -235,137 +228,171 @@
     def to_core(k):
         return remote(c_out, c_in.at[lax.rem(k, 2)], c_sem.at[0], c_sem.at[1 + lax.rem(k, 2)], s=other)
 
-    def to_x(k):
-        return remote(x_out, x_in.at[lax.rem(k, 2)], x_sem.at[0], x_sem.at[1 + lax.rem(k, 2)], s=across)
-
-    def to_y(k):
-        return remote(y_out, y_in.at[lax.rem(k, 2)], y_sem.at[0], y_sem.at[1 + lax.rem(k, 2)], r=by_y)
-
-    def to_z(k):
-        return remote(z_out, z_in.at[lax.rem(k, 2)], z_sem.at[0], z_sem.at[1 + lax.rem(k, 2)], r=by_z)
-
-    def finals(k):
+    def cols(p):
+        return pl.ds(p * chunk, chunk)
+
+    def hop(out, into, sem, k, p, **where):
+        return remote(out.at[:, cols(p)], into.at[lax.rem(k, 2), :, cols(p)], sem.at[p, 0], sem.at[p, 1 + lax.rem(k, 2)], **where)
+
+    def to_x(k, p):
+        return hop(c_out.at[0], x_in, x_sem, k, p, s=across)
+
+    def to_y(k, p):
+        return hop(y_out, y_in, y_sem, k, p, r=by_y)
+
+    def to_z(k, p):
+        return hop(z_out, z_in, z_sem, k, p, r=by_z)
+
+    def core_done(k):
+        to_core(k).wait()
+        c_out[0] = (mine[1 - x] + c_in[lax.rem(k, 2), 1 - x].astype(F32)).astype(BF16)
+        for p in range(3):
+            to_x(k, p).start()
+        mine[x] += c_in[lax.rem(k, 2), x].astype(F32)
+
+    def x_done(k, p):
+        to_x(k, p).wait()
+        y_out[:, cols(p)] = (mine[x, :, cols(p)] + x_in[lax.rem(k, 2), :, cols(p)].astype(F32)).astype(BF16)
+        to_y(k, p).start()
+
+    def y_done(k, p):
+        to_y(k, p).wait()
+        end_final(k - 1, p)
+        z_out[:, cols(p)] = (y_out[:, cols(p)].astype(F32) + y_in[lax.rem(k, 2), :, cols(p)].astype(F32)).astype(BF16)
+        to_z(k, p).start()
+
+    def z_done(k, p):
+        to_z(k, p).wait()
+        z_out[:, cols(p)] = (z_out[:, cols(p)].astype(F32) + z_in[lax.rem(k, 2), :, cols(p)].astype(F32)).astype(BF16)
+        start_final(k, p)
+
+    def final(k, p):
         layer, of = 1 - lax.div(k, chunks), lax.rem(k, chunks)
-        cols = pl.ds(pl.multiple_of(of * chunk, 128), chunk)
+        if p < 2:
+            to = (gg, gu)[p].at[layer, :, pl.ds(pl.multiple_of(of * chunk, 128), chunk)]
+            return True, pltpu.make_async_copy(z_out.at[:, cols(p)], to, l_sem.at[p]), None
         number = 4 * of + s
         owner, place = lax.div(number, chunks), lax.rem(number, chunks)
         to = gd.at[layer, pl.ds(pl.multiple_of(place * n, 16), n)]
-        down = done.at[:, pl.ds(2 * chunk, d)]
-        here = [
-            pltpu.make_async_copy(done.at[:, pl.ds(0, chunk)], gg.at[layer, :, cols], l_sem.at[0]),
-            pltpu.make_async_copy(done.at[:, pl.ds(chunk, chunk)], gu.at[layer, :, cols], l_sem.at[1]),
-        ]
-        return here, owner == s, pltpu.make_async_copy(down, to, l_sem.at[2]), remote(down, to, d_send, d_recv.at[layer, place], s=owner)
-
-    def start_finals(k):
-        here, stays, local, away = finals(k)
-        for copy in here:
-            copy.start()
-        pl.when(stays)(local.start)
-        pl.when(jnp.logical_not(stays))(away.start)
-
-    def end_finals(k):
-        here, stays, local, away = finals(k)
-        for copy in here:
-            copy.wait()
-        pl.when(stays)(local.wait)
-        pl.when(jnp.logical_not(stays))(away.wait_send)
+        return owner == s, pltpu.make_async_copy(z_out.at[:, cols(p)], to, l_sem.at[p]), remote(z_out.at[:, cols(p)], to, d_send, d_recv.at[layer, place], s=owner)
+
+    def start_final(k, p):
+        stays, local, away = final(k, p)
+        if away is None:
+            local.start()
+        else:
+            pl.when(stays)(local.start)
+            pl.when(jnp.logical_not(stays))(away.start)
+
+    def end_final(k, p):
+        stays, local, away = final(jnp.maximum(k, 0), p)
+        pl.when((k >= 0) & stays)(local.wait)
+        if away is not None:
+            pl.when((k >= 0) & jnp.logical_not(stays))(away.wait_send)
 
     @pl.when((c == 0) & (t == 0))
     def _():
+        load = pltpu.make_async_copy(dy_ref, dy_s, l_sem.at[0])
+        load.start()
         greet({"s": other}, {"s": across}, {"s": 3 - s}, {"r": by_y}, {"r": by_z})
+        load.wait()
 
     @pl.when((t == 1) & (c >= 2))
     def _():
-        k = c - 2
-        to_y(k).wait()
-        z_out[...] = (y_out[...].astype(F32) + y_in[lax.rem(k, 2)].astype(F32)).astype(BF16)
-        to_z(k).start()
-
-    @pl.when((t == 1) & (c >= 1) & (c <= last + 1))
-    def _():
-        k = c - 1
-        to_core(k).wait()
-        x_out[...] = (mine[1 - x] + c_in[lax.rem(k, 2), 1 - x].astype(F32)).astype(BF16)
-        to_x(k).start()
-        mine[x] += c_in[lax.rem(k, 2), x].astype(F32)
-
-    @pl.when((t == 3) & (c >= 2))
-    def _():
-        k = c - 2
-        to_z(k).wait()
-        pl.when(k >= 1)(lambda: end_finals(k - 1))
-        done[...] = (z_out[...].astype(F32) + z_in[lax.rem(k, 2)].astype(F32)).astype(BF16)
-        start_finals(k)
-
-    @pl.when((t == 3) & (c >= 1) & (c <= last + 1))
-    def _():
-        k = c - 1
-        to_x(k).wait()
-        y_out[...] = (mine[x] + x_in[lax.rem(k, 2)].astype(F32)).astype(BF16)
-        to_y(k).start()
+        y_done(c - 2, 0)
+        y_done(c - 2, 1)
+
+    @pl.when((t == 1) & (c >= 1))
+    def _():
+        core_done(c - 1)
+
+    @pl.when((t == 2) & (c >= 2))
+    def _():
+        y_done(c - 2, 2)
+
+    @pl.when((t == steps - 1) & (c >= 1))
+    def _():
+        x_done(c - 1, 0)
+        x_done(c - 1, 1)
+
+    load_x = pltpu.make_async_copy(x_ref.at[rows], a_s.at[rows], r_sem.at[t])
 
     @pl.when(c == 0)
     def _():
         wide = h_ref[...].astype(F32)
         a_s[rows] = (wide * scale_of(wide)).astype(BF16)
-        dy_s[rows] = dy_ref[...]
-        da_s[rows] = jnp.zeros((block, d), F32)
+        da_s[:, rows] = jnp.zeros((d, block), F32)
 
     @pl.when(c == chunks)
     def _():
-        wide = x_ref[...].astype(F32)
+        load_x.wait()
+        wide = a_s[rows].astype(F32)
         a_s[rows] = (wide * scale_of(wide)).astype(BF16)
 
-    @pl.when(c <= last)
-    def _():
-        @pl.when(t == 0)
+    @pl.when(t == 0)
+    def _():
+        acc_s[...] = jnp.zeros_like(acc_s)
+
+    for i in range(block // sub):
+        at = pl.ds(pl.multiple_of(t * block + i * sub, sub), sub)
+        a, dy = a_s[at], dy_s[at]
+        both = dot(a, wgu_ref[0], 1, 0)
+        dh = dot(dy, wd_ref[0], 1, 1).astype(BF16).astype(F32)
+        g, u = both[:, :chunk], both[:, chunk:]
+        sg = sigmoid(g)
+        sl = g * sg
+        hid = (sl * u).astype(BF16)
+        by_u = (dh * sl).astype(BF16)
+        by_g = (dh * u * (sg * (1 + g * (1 - sg)))).astype(BF16)
+        by_gu = jnp.concatenate([by_g, by_u], 1)
+        acc_s[:, : 2 * chunk] += dot(a, by_gu, 0, 0)
+        acc_s[:, 2 * chunk :] += dot(hid, dy, 0, 0)
+
+        @pl.when(c < chunks)
         def _():
-            acc_s[...] = jnp.zeros_like(acc_s)
-
-        for i in range(block // sub):
-            at = pl.ds(pl.multiple_of(t * block + i * sub, sub), sub)
-            a, dy = a_s[at], dy_s[at]
-            both = dot(a, wgu_ref[0], 1, 0)
-            dh = dot(dy, wd_ref[0], 1, 1).astype(BF16).astype(F32)
-            g, u = both[:, :chunk], both[:, chunk:]
-            sg = sigmoid(g)
-            sl = g * sg
-            hid = (sl * u).astype(BF16)
-            by_u = (dh * sl).astype(BF16)
-            by_g = (dh * u * (sg * (1 + g * (1 - sg)))).astype(BF16)
-            by_gu = jnp.concatenate([by_g, by_u], 1)
-            acc_s[:, : 2 * chunk] += dot(a, by_gu, 0, 0)
-            acc_s[:, 2 * chunk :] += dot(hid, dy, 0, 0)
-
-            @pl.when(c < chunks)
-            def _():
-                da_s[at] += dot(by_gu, wgu_ref[0], 1, 1)
-
-        @pl.when(c == chunks - 1)
-        def _():
-            da = da_s[rows].astype(BF16).astype(F32)
-            wide = h_ref[...].astype(F32)
-            scale = scale_of(wide)
-            along = jnp.sum(da * wide, -1, keepdims=True) * (scale * scale * scale) * (1.0 / d)
-            dy_s[rows] = (dy_s[rows].astype(F32) + (da * scale - wide * along).astype(BF16).astype(F32)).astype(BF16)
-
-        @pl.when(t == steps - 1)
-        def _():
-            for i in range(2):
-                mine[i] = acc_s[pl.ds(pl.multiple_of((2 * i + core) * n, 8), n)]
-                c_out[i] = acc_s[pl.ds(pl.multiple_of((2 * i + 1 - core) * n, 8), n)].astype(BF16)
-            to_core(c).start()
-
-    @pl.when((c == last + 2) & (t == steps - 1))
-    def _():
-        end_finals(last)
+            da_s[:, at] += dot(wgu_ref[0], by_gu, 1, 1)
+
+    @pl.when(c == chunks - 1)
+    def _():
+        load_x.start()
+        da = da_s[:, rows].T.astype(BF16).astype(F32)
+        wide = h_ref[...].astype(F32)
+        scale = scale_of(wide)
+        along = jnp.sum(da * wide, -1, keepdims=True) * (scale * scale * scale) * (1.0 / d)
+        dy_s[rows] = (dy_s[rows].astype(F32) + (da * scale - wide * along).astype(BF16).astype(F32)).astype(BF16)
+
+    @pl.when((t == steps - 1) & (c >= 1))
+    def _():
+        x_done(c - 1, 2)
+
+    @pl.when((t == steps - 1) & (c >= 2))
+    def _():
+        for p in range(3):
+            z_done(c - 2, p)
+
+    @pl.when(t == steps - 1)
+    def _():
+        for i in range(2):
+            mine[i] = acc_s[pl.ds(pl.multiple_of((2 * i + core) * n, 8), n)]
+            c_out[i] = acc_s[pl.ds(pl.multiple_of((2 * i + 1 - core) * n, 8), n)].astype(BF16)
+        to_core(c).start()
+
+    @pl.when((c == last) & (t == steps - 1))
+    def _():
+        core_done(last)
+        for do, k, p in (
+            (y_done, 1, 0), (y_done, 1, 1), (x_done, 0, 0), (y_done, 1, 2), (x_done, 0, 1), (z_done, 1, 0), (z_done, 1, 1), (x_done, 0, 2),
+            (y_done, 0, 0), (z_done, 1, 2), (y_done, 0, 1), (y_done, 0, 2), (z_done, 0, 0), (z_done, 0, 1), (z_done, 0, 2),
+        ):
+            do(last - k, p)
+        for p in range(3):
+            end_final(last, p)
         for layer in range(2):
             for place in range(chunks):
                 number = s * chunks + place
                 to = gd.at[layer, pl.ds(place * n, n)]
                 from_other = lax.rem(number, 4) != s
-                copy = remote(done.at[:, pl.ds(2 * chunk, d)], to, d_send, d_recv.at[layer, place], s=other)
+                copy = remote(z_out.at[:, pl.ds(2 * chunk, d)], to, d_send, d_recv.at[layer, place], s=other)
                 pl.when(from_other)(copy.wait_recv)
 
 
@@ -379,11 +406,11 @@
     at = lambda *when: pl.BlockSpec((block, d), lambda c, t: (jnp.where(functools.reduce(jnp.logical_or, [c == w for w in when]), t, 0), 0))
     return pl.pallas_call(
         functools.partial(backward_kernel, sizes),
-        grid=(last + 3, tokens // block),
+        grid=(last + 1, tokens // block),
         in_specs=[
             at(0, chunks - 1),
-            at(0),
-            at(chunks),
+            pl.BlockSpec(memory_space=pl.ANY),
+            pl.BlockSpec(memory_space=pl.ANY),
             pl.BlockSpec((1, d, 2 * chunk), lambda c, t: (jnp.minimum(c, last), 0, 0)),
             pl.BlockSpec((1, chunk, d), lambda c, t: (lax.div(jnp.minimum(c, last), chunks), lax.rem(jnp.minimum(c, last), chunks), 0)),
         ],
@@ -396,25 +423,24 @@
         scratch_shapes=[
             pltpu.VMEM((tokens, d), BF16),
             pltpu.VMEM((tokens, d), BF16),
-            pltpu.VMEM((tokens, d), F32),
+            pltpu.VMEM((d, tokens), F32),
             pltpu.VMEM((d, wide), F32),
             pltpu.VMEM((2, n, wide), F32),
             pltpu.VMEM((2, n, wide), BF16),
             pltpu.VMEM((2, 2, n, wide), BF16),
-            pltpu.VMEM((n, wide), BF16),
             pltpu.VMEM((2, n, wide), BF16),
             pltpu.VMEM((n, wide), BF16),
             pltpu.VMEM((2, n, wide), BF16),
             pltpu.VMEM((n, wide), BF16),
             pltpu.VMEM((2, n, wide), BF16),
-            pltpu.VMEM((n, wide), BF16),
             dma((3,)),
-            dma((3,)),
-            dma((3,)),
-            dma((3,)),
+            dma((3, 3)),
+            dma((3, 3)),
+            dma((3, 3)),
             dma,
             dma((2, chunks)),
             dma((3,)),
+            dma((tokens // block,)),
         ],
         compiler_params=pltpu.CompilerParams(collective_id=1, has_side_effects=True, vmem_limit_bytes=VMEM_LIMIT),
         name="backward",
@@ -432,8 +458,8 @@
     def step(x, dy, *arrays):
         weights, m, v = (arrays[i : i + 3] for i in (0, 3, 6))
         x, dy = x[0], dy[0]
-        h, wgu, wd = forward(x, *weights, 640, 1024)
-        gradients = backward(h, dy, x, wgu, wd, 640, 1024, 512)
+        h, wgu, wd = forward(x, *weights, 640, 1024, 512)
+        gradients = backward(h, dy, x, wgu, wd, 640, 1024, 1024)
         new = [adamw(w.astype(F32), m, v, g.astype(F32)) for w, m, v, g in zip(weights, m, v, gradients, strict=True)]
         return tuple(one[which] for which in range(3) for one in new)
 

time: 539 us -> 489 us (0.907)
  Pallas kernels: 515 us -> 465 us
    pallas_call x1, Pallas kernels: 394 us -> 358 us  [backward(): pl.pallas_call(functools.partial(backward_kernel, sizes), grid=(last + 1,...]
    pallas_call x1, Pallas kernels: 122 us -> 107 us  [forward(): pl.pallas_call(functools.partial(forward_kernel, sizes), grid=(chunks + 1...]
where the time goes in v2:
time: 489 us
  Pallas kernels  465 us (95%)
  other arithmetic  20.6 us (4%)
    pallas_call x1, Pallas kernels, backward(): pl.pallas_call(functools.partial(backward_kernel, sizes), grid=(last + 1,...  358 us
    pallas_call x1, Pallas kernels, forward(): pl.pallas_call(functools.partial(forward_kernel, sizes), grid=(chunks + 1...  107 us
    convert_element_type x2, other arithmetic, adamw(): return ((w - 0.02 * step).astype(BF16), m, v)  20.6 us

profile of v2, /device:TPU:0, one launch (start us, length us, event | category | flops | bytes accessed | tf_op | source)
XLA Modules:
  0.0 488.9 jit_solution(10667138742311321913)
XLA Ops:
  0.6 106.9 %forward.1 = (bf16[4096,640]{1,0:T(8,128)(2,1)}, bf16[10,640,1280]{2,1,0:T(8,128)(2,1)}, bf16[2,3200,640]{2,1,0:T(8,128)(2,1)}) custom-call(bf16[4096,640]{1,0:T(8,128)(2,1)} %bitcast.2, bf16[2,160,3200]{2,1,0:T(8,128)(2,1)} %wg_ref.1, bf16[2,160,3200]{2,1,0:T(8,128)(2,1)} %wu_ref.1, bf16[2,800,640]{2,1,0:T(8,128)(2,1)} %wd_ref.1), custom_call_target="tpu_custom_call" | custom-call | tf_op jit(solution)/shard_map/forward/pallas_call | solution.py:185
  107.6 358.3 %backward.1 = (bf16[2,160,3200]{2,1,0:T(8,128)(2,1)}, bf16[2,160,3200]{2,1,0:T(8,128)(2,1)}, bf16[2,800,640]{2,1,0:T(8,128)(2,1)}) custom-call(bf16[4096,640]{1,0:T(8,128)(2,1)} %get-tuple-element.15.h_ref, bf16[4096,640]{1,0:T(8,128)(2,1)} %bitcast.4, bf16[4096,640]{1,0:T(8,128)(2,1)} %bitcast.3, bf16[10,640,1280]{2,1,0:T(8,128)(2,1)} %get-tuple-element.16.wgu_ref, ...), custom_call_target="tpu_custom_call" | custom-call | tf_op jit(solution)/shard_map/backward/pallas_call | solution.py:407
  465.9 0.0 copy-start
  465.9 0.0 copy-start.1
  465.9 0.0 copy-start.2
  466.0 0.0 copy-start.3
  466.0 8.9 %fusion.10 = (bf16[2,800,640]{2,1,0:T(8,128)(2,1)}, f32[2,800,640]{2,1,0:T(8,128)}, f32[2,800,640]{2,1,0:T(8,128)}) fusion(bf16[2,800,640]{2,1,0:T(8,128)(2,1)} %wd_ref.1, bf16[2,800,640]{2,1,0:T(8,128)(2,1)} %get-tuple-element.20, f32[2,800,640]{2,1,0:T(8,128)} %param.21, f32[2,800,640]{2,1,0:T(8,128)} %param.18), kind=kLoop, calls=%fused_computation.22 | loop fusion | flops 16384000 | bytes 22528000 | tf_op jit(solution)/shard_map/convert_element_type | solution.py:454
  474.8 0.0 copy-done
  474.8 0.0 copy-done.1
  474.8 1.8 copy-done.2
  476.6 0.6 copy-done.3
  477.2 11.7 %fusion.2 = (bf16[2,160,3200]{2,1,0:T(8,128)(2,1)}, f32[2,160,3200]{2,1,0:T(8,128)}, f32[2,160,3200]{2,1,0:T(8,128)}, bf16[2,160,3200]{2,1,0:T(8,128)(2,1)}, f32...) fusion(bf16[2,160,3200]{2,1,0:T(8,128)(2,1)S(1)} %copy-done, bf16[2,160,3200]{2,1,0:T(8,128)(2,1)S(1)} %copy-done.3, ...), kind=kLoop, calls=%fused_computation.14 | loop fusion | flops 32768000 | bytes 45056000 | tf_op jit(solution)/shard_map/convert_element_type | solution.py:454
Async XLA Ops:
  465.9 8.9 %copy-start = (bf16[2,160,3200]{2,1,0:T(8,128)(2,1)S(1)}, bf16[2,160,3200]{2,1,0:T(8,128)(2,1)}, u32[]{:S(2)}) copy-start(bf16[2,160,3200]{2,1,0:T(8,128)(2,1)} %wg_ref.1) | copy-start | bytes 6144004
  465.9 8.9 %copy-start.1 = (bf16[2,160,3200]{2,1,0:T(8,128)(2,1)S(1)}, bf16[2,160,3200]{2,1,0:T(8,128)(2,1)}, u32[]{:S(2)}) copy-start(bf16[2,160,3200]{2,1,0:T(8,128)(2,1)} %wu_ref.1) | copy-start | bytes 6144004
  465.9 10.7 %copy-start.2 = (f32[2,160,3200]{2,1,0:T(8,128)S(1)}, f32[2,160,3200]{2,1,0:T(8,128)}, u32[]{:S(2)}) copy-start(f32[2,160,3200]{2,1,0:T(8,128)} %param.19) | copy-start | bytes 12288004
  466.0 11.2 %copy-start.3 = (bf16[2,160,3200]{2,1,0:T(8,128)(2,1)S(1)}, bf16[2,160,3200]{2,1,0:T(8,128)(2,1)}, u32[]{:S(2)}) copy-start(bf16[2,160,3200]{2,1,0:T(8,128)(2,1)} %get-tuple-element.18) | copy-start | bytes 6144004
